TPU v7x, 256 devices: a whole 4x4x8 slice. The times are simulated.
256 devices in a mesh: row: 8 (over z_hi, y), col: 32 (over z_lo, x, core).
Axes of the slice: x: 4, y: 4, z: 8 (z_hi: 2, z_lo: 4; z = z_hi * 4 + z_lo), core: 2. Of those that a mesh axis runs over, the one named last changes fastest.
Arguments:
- positions: float32 [3, 262144], P(None, ('row', 'col')), may hold values from -6 to 6
- types: int32 [262144], P(('row', 'col')), may hold values from 0 to 4
- radius_type: float32 [5], replicated, may hold values from 0.6 to 1.2
- valence_type: float32 [5], replicated, may hold values from 5 to 60
- bond_depth: float32 [5, 5], replicated, may hold values from 0.02 to 0.2
- pair_tiles: int32 [8, 32, 96, 2], P('row', 'col'), may hold values from 0 to 255, as said below
- tile_count: int32 [8, 32], P('row', 'col'), may hold values from 24 to 96, as said below
Outputs:
- force_energy: float32 [4, 262144], P(None, ('row', 'col'))
Inputs may be any that keep to these rules, and one draw needn't show every extreme that they name: `pair_tiles`: each entry is (a, b) with a below 256 and b below 64; the 96 tiles of one device are distinct. Only the first tile_count[r, c] tiles of device (r, c) are live; the most, 96, is reached on some device in every draw.
All inputs are finite; a program needn't handle non-finite values.
Results may differ from a plain program's by a relative error of at most 0.0003.
Values sent between devices are 32-bit elements; how exact they have to be, the bound alone decides.
A program may use at most 64 MiB of HBM per device.

v0:
```python
import functools

import jax
import jax.numpy as jnp
from jax import lax
from jax.experimental import pallas as pl
from jax.experimental.pallas import tpu as pltpu
from jax.sharding import PartitionSpec as P

TILE = 128
SLOTS = 96
CHIPS = 16
CHUNK = 32
MESH = pl.DeviceIdType.MESH
F32 = jnp.float32


def pieces(value):
    high = value.astype(jnp.bfloat16)
    rest = value - high.astype(F32)
    middle = rest.astype(jnp.bfloat16)
    low = (rest - middle.astype(F32)).astype(jnp.bfloat16)
    return high, middle, low


def by_type(types, table):
    value = jnp.full(types.shape, table[0], F32)
    for t in range(1, len(table)):
        value = jnp.where(types == F32(t), table[t], value)
    return value


def kernel(
    pos_ref, types_ref, radius_ref, valence_ref, depth_ref, tiles_ref, count_ref, out_ref,
    rows, cols, row_radius, row_u, col_u, col_t, col_ub, onehot, parts, store,
    coord_part, coord_in, coord_sum, coord_rx, force_part, force_in, force_sum, force_rx,
    row_send, row_recv, col_send, col_recv, pair_send, pair_recv,
    c_send, c_recv, u_send, u_recv, v_send, v_recv, f_send, f_recv,
):
    r = lax.axis_index("row")
    c = lax.axis_index("col")
    core = lax.rem(c, 2)
    q = c // 2
    z, x = q // 4, lax.rem(q, 4)
    zh, y = r // 4, lax.rem(r, 4)
    other = 1 - core

    def copy(src, dst, send, recv, row, col):
        return pltpu.make_async_remote_copy(
            src_ref=src, dst_ref=dst, send_sem=send, recv_sem=recv,
            device_id=(row, col), device_id_type=MESH,
        )

    chips = [lax.rem(q + k, CHIPS) for k in range(1, CHIPS)]
    rows_of = [lax.rem(r + k, 8) for k in range(1, 8)]

    barrier = pltpu.get_barrier_semaphore()
    for p in chips:
        pl.semaphore_signal(barrier, inc=1, device_id=(r, p * 2 + core), device_id_type=MESH)
    for p in rows_of:
        pl.semaphore_signal(barrier, inc=1, device_id=(p, c), device_id_type=MESH)
    pl.semaphore_signal(barrier, inc=1, device_id=(r, q * 2 + other), device_id_type=MESH)

    own_types = types_ref[...].astype(F32)
    for k in range(8):
        piece = pos_ref[:, k * TILE : (k + 1) * TILE]
        for d in range(3):
            rows[core, q, d, k : k + 1, :] = piece[d : d + 1]
            cols[r, d, k : k + 1, :] = piece[d : d + 1]
    rows[core, q, 3] = own_types
    cols[r, 3] = own_types

    pl.semaphore_wait(barrier, CHIPS - 1 + 7 + 1)

    started = []

    def go(*args):
        descriptor = copy(*args)
        descriptor.start()
        started.append(descriptor)

    def send_row(origin, row, col, slot):
        block = rows.at[core, origin]
        go(block, block, row_send.at[slot], row_recv.at[core, origin], row, col)

    def send_col(origin, row, slot):
        block = cols.at[origin]
        go(block, block, col_send.at[slot], col_recv.at[origin], row, c)

    def device(zz, xx):
        return (zz * 4 + xx) * 2 + core

    far = [lax.rem(z + k, 4) for k in range(1, 4)]
    side = [lax.rem(x + k, 4) for k in range(1, 4)]
    yy = [lax.rem(y + k, 4) for k in range(1, 4)]
    partner = q * 2 + other
    twin = (1 - zh) * 4 + y
    slot = 0
    send_col(r, twin, 0)
    for zz in far:
        send_row(q, r, device(zz, x), slot)
        slot += 1
    for xx in side:
        send_row(q, r, device(z, xx), slot)
        slot += 1
    for k, near in enumerate(yy):
        send_col(r, zh * 4 + near, 1 + k)
    send_row(q, r, partner, slot)
    slot += 1

    def row_wait(par, origin):
        block = rows.at[par, origin]
        copy(block, block, row_send.at[0], row_recv.at[par, origin], r, partner).wait_recv()

    def col_wait(origin):
        block = cols.at[origin]
        copy(block, block, col_send.at[0], col_recv.at[origin], twin, c).wait_recv()

    live = count_ref[0]
    lane = lax.broadcasted_iota(jnp.int32, (8, TILE), 1) // 8
    target = lax.broadcasted_iota(jnp.int32, (256, TILE), 0)
    for m in range(SLOTS // 16):

        def pick(s, held, m=m):
            at = m * 16 + s
            a = tiles_ref[2 * at]
            place = ((a >> 3) & 1) * 128 + (a >> 4) * 8 + (a & 7)
            place = jnp.where(at < live, place, -1)
            return jnp.where(lane == s, place, held)

        held = lax.fori_loop(0, 16, pick, jnp.full((8, TILE), -1, jnp.int32))
        match = target == held[0:1]
        onehot[:, m * TILE : (m + 1) * TILE] = jnp.where(match, F32(1), F32(0)).astype(jnp.bfloat16)

    for zz in far:
        origin = zz * 4 + x
        row_wait(core, origin)
        for xx in side:
            send_row(origin, r, device(z, xx), slot)
            slot += 1
        send_row(origin, r, partner, slot)
        slot += 1
    col_wait(twin)
    for k, near in enumerate(yy):
        send_col(twin, zh * 4 + near, 4 + k)
    for xx in side:
        for k in range(4):
            origin = lax.rem(z + k, 4) * 4 + xx
            row_wait(core, origin)
            send_row(origin, r, partner, slot)
            slot += 1
    for near in yy:
        col_wait(zh * 4 + near)
        col_wait((1 - zh) * 4 + near)

    radius = [radius_ref[t] * F32(0.5) for t in range(5)]
    valence = [valence_ref[t] for t in range(5)]
    for g in range(8):
        kinds = cols[g, 3]
        feats = [cols[g, 0], cols[g, 1], cols[g, 2], by_type(kinds, radius), by_type(kinds, valence)]
        for t in range(5):
            feats.append(by_type(kinds, [depth_ref[5 * t + u] for u in range(5)]))
        while len(feats) < 16:
            feats.append(jnp.zeros((8, TILE), F32))
        turned = jnp.concatenate(feats, axis=0).T
        for k in range(8):
            col_t[g * 8 + k] = turned if k == 0 else pltpu.roll(turned, TILE - k, 1)

    for p in range(CHIPS):
        row_wait(other, p)
    for par in range(2):
        for p in range(CHIPS):
            row_radius[par, p] = by_type(rows[par, p, 3], radius)

    ones_row = lax.broadcasted_iota(jnp.int32, (8, TILE), 0) == 0

    def tile_of(s):
        a = tiles_ref[2 * s]
        b = tiles_ref[2 * s + 1]
        same = (b // 8 == r) & (a // 8 == c) & ((a & 7) == (b & 7))
        return (a >> 3) & 1, a >> 4, a & 7, b, jnp.where(same, F32(1), F32(0))

    def near_row(ref, sp, sq, d, sb):
        return ref[sp, sq, d, pl.ds(sb, 1), :]

    def fold(value):
        return jnp.sum(value.reshape(-1, 8, TILE), axis=0)

    def first(s, carry):
        sp, sq, sb, b, same = tile_of(s)
        near = [near_row(rows, sp, sq, d, sb) for d in range(3)]
        near_r = row_radius[sp, sq, pl.ds(sb, 1), :]
        total = jnp.where(ones_row, -same, F32(0))
        for k in range(TILE // CHUNK):
            far_t = col_t[b, k * CHUNK : (k + 1) * CHUNK, :]
            dist = F32(0)
            for d in range(3):
                offset = near[d] - far_t[:, 8 * d : 8 * d + 1]
                dist = dist + offset * offset
            rho = near_r + far_t[:, 24:25]
            ratio = dist / (rho * rho)
            total = total + fold(jnp.exp(-(ratio * ratio * ratio)))
        parts[0, pl.ds(pl.multiple_of(s * 8, 8), 8), :] = total
        return carry

    lax.fori_loop(0, SLOTS, first, 0)

    def scatter(f):
        total = None
        for piece in pieces(parts[f]):
            term = jnp.dot(onehot[...], piece, preferred_element_type=F32)
            total = term if total is None else total + term
        return total.reshape(2, CHIPS, 8, TILE)

    coord_part[...] = scatter(0)
    go(coord_part.at[other], coord_in, pair_send.at[0], pair_recv.at[0], r, partner)
    mine = coord_part[core]
    copy(coord_part.at[0], coord_in, pair_send.at[0], pair_recv.at[0], r, partner).wait_recv()
    coord_sum[...] = mine + coord_in[...]
    for k, p in enumerate(chips):
        go(coord_sum.at[p], coord_rx.at[q], c_send.at[k], c_recv.at[q], r, p * 2 + core)

    diagonal = [
        jnp.where(
            lax.broadcasted_iota(jnp.int32, (CHUNK, TILE), 0) + k * CHUNK
            == lax.broadcasted_iota(jnp.int32, (CHUNK, TILE), 1),
            F32(1),
            F32(0),
        )
        for k in range(TILE // CHUNK)
    ]

    def prepare(s, carry):
        sp, sq, sb, b, same = tile_of(s)
        near = [near_row(rows, sp, sq, d, sb) for d in range(3)]
        near_r = row_radius[sp, sq, pl.ds(sb, 1), :]
        kinds = near_row(rows, sp, sq, 3, sb)
        near_v = by_type(kinds, valence)
        for k in range(TILE // CHUNK):
            far_t = col_t[b, k * CHUNK : (k + 1) * CHUNK, :]
            offsets = [near[d] - far_t[:, 8 * d : 8 * d + 1] for d in range(3)]
            dist = offsets[0] * offsets[0] + offsets[1] * offsets[1] + offsets[2] * offsets[2]
            rho = near_r + far_t[:, 24:25]
            inverse = F32(1) / (rho * rho)
            ratio = dist * inverse
            square = ratio * ratio
            bond = jnp.exp(-(square * ratio))
            depth = jnp.broadcast_to(far_t[:, 40:41], (CHUNK, TILE))
            for t in range(1, 5):
                depth = jnp.where(kinds == F32(t), far_t[:, 40 + 8 * t : 41 + 8 * t], depth)
            numer = depth * (near_v + far_t[:, 32:33]) * bond
            numer = numer * (F32(1) - same * diagonal[k])
            pull = F32(6) * numer * square * inverse
            at = slice(k * CHUNK, (k + 1) * CHUNK)
            for d in range(3):
                store[s, d, at, :] = pull * offsets[d]
            store[s, 3, at, :] = numer
        return carry

    lax.fori_loop(0, SLOTS // 2, prepare, 0)

    own = coord_sum[q]
    for p in chips:
        copy(coord_sum.at[0], coord_rx.at[p], c_send.at[0], c_recv.at[p], r, p * 2 + core).wait_recv()
        own = own + coord_rx[p]
    own = own + by_type(rows[core, q, 3], valence)
    row_u[core, q] = own
    col_u[r] = own
    for k, p in enumerate(rows_of):
        go(col_u.at[r], col_u.at[r], v_send.at[k], v_recv.at[r], p, c)
    for k, p in enumerate(chips):
        go(row_u.at[core, q], row_u.at[core, q], u_send.at[k], u_recv.at[q], r, p * 2 + core)

    lax.fori_loop(SLOTS // 2, SLOTS, prepare, 0)

    for p in chips:
        block = row_u.at[core, p]
        copy(block, block, u_send.at[0], u_recv.at[p], r, p * 2 + core).wait_recv()
    go(row_u.at[core], row_u.at[core], pair_send.at[1], pair_recv.at[1], r, partner)
    for p in rows_of:
        copy(col_u.at[p], col_u.at[p], v_send.at[0], v_recv.at[p], p, c).wait_recv()
    turned = col_u[...].reshape(64, TILE).T
    for b in range(64):
        col_ub[b] = jnp.broadcast_to(turned[:, b : b + 1], (TILE, TILE))
    copy(row_u.at[other], row_u.at[other], pair_send.at[1], pair_recv.at[1], r, partner).wait_recv()

    def second(s, carry):
        sp, sq, sb, b, unused = tile_of(s)
        near_u = row_u[sp, sq, pl.ds(sb, 1), :]
        total = [jnp.zeros((8, TILE), F32) for d in range(4)]
        for k in range(TILE // CHUNK):
            at = slice(k * CHUNK, (k + 1) * CHUNK)
            scale = F32(1) / (near_u + col_ub[b, at, :])
            for d in range(4):
                total[d] = total[d] - fold(store[s, d, at, :] * scale)
        for d in range(4):
            parts[d, pl.ds(pl.multiple_of(s * 8, 8), 8), :] = total[d]
        return carry

    lax.fori_loop(0, SLOTS, second, 0)

    for d in range(4):
        force_part[:, :, d] = scatter(d)
    go(force_part.at[other], force_in, pair_send.at[2], pair_recv.at[2], r, partner)
    copy(force_part.at[0], force_in, pair_send.at[2], pair_recv.at[2], r, partner).wait_recv()
    force_sum[...] = force_part[core] + force_in[...]
    for k, p in enumerate(chips):
        go(force_sum.at[p], force_rx.at[q], f_send.at[k], f_recv.at[q], r, p * 2 + core)
    own = force_sum[q]
    for p in chips:
        copy(force_sum.at[0], force_rx.at[p], f_send.at[0], f_recv.at[p], r, p * 2 + core).wait_recv()
        own = own + force_rx[p]
    for k in range(8):
        out_ref[:, k * TILE : (k + 1) * TILE] = own[:, k, :]
    for descriptor in started:
        descriptor.wait_send()


def local(positions, types, radius_type, valence_type, bond_depth, pair_tiles, tile_count):
    vmem = pl.BlockSpec(memory_space=pltpu.VMEM)
    smem = pl.BlockSpec(memory_space=pltpu.SMEM)
    dma = pltpu.SemaphoreType.DMA
    return pl.pallas_call(
        kernel,
        out_shape=jax.ShapeDtypeStruct((4, positions.shape[1]), F32),
        in_specs=[vmem, vmem, smem, smem, smem, smem, smem],
        out_specs=vmem,
        scratch_shapes=[
            pltpu.VMEM((2, CHIPS, 4, 8, TILE), F32),
            pltpu.VMEM((8, 4, 8, TILE), F32),
            pltpu.VMEM((2, CHIPS, 8, TILE), F32),
            pltpu.VMEM((2, CHIPS, 8, TILE), F32),
            pltpu.VMEM((8, 8, TILE), F32),
            pltpu.VMEM((64, TILE, TILE), F32),
            pltpu.VMEM((64, TILE, TILE), F32),
            pltpu.VMEM((256, 8 * SLOTS), jnp.bfloat16),
            pltpu.VMEM((4, 8 * SLOTS, TILE), F32),
            pltpu.VMEM((SLOTS, 4, TILE, TILE), F32),
            pltpu.VMEM((2, CHIPS, 8, TILE), F32),
            pltpu.VMEM((CHIPS, 8, TILE), F32),
            pltpu.VMEM((CHIPS, 8, TILE), F32),
            pltpu.VMEM((CHIPS, 8, TILE), F32),
            pltpu.VMEM((2, CHIPS, 4, 8, TILE), F32),
            pltpu.VMEM((CHIPS, 4, 8, TILE), F32),
            pltpu.VMEM((CHIPS, 4, 8, TILE), F32),
            pltpu.VMEM((CHIPS, 4, 8, TILE), F32),
            dma((31,)), dma((2, CHIPS)), dma((7,)), dma((8,)), dma((3,)), dma((3,)),
            dma((15,)), dma((CHIPS,)), dma((15,)), dma((CHIPS,)), dma((7,)), dma((8,)),
            dma((15,)), dma((CHIPS,)),
        ],
        compiler_params=pltpu.CompilerParams(
            collective_id=0, has_side_effects=True, vmem_limit_bytes=60 * 1024 * 1024
        ),
    )(
        positions,
        types.reshape(8, TILE),
        radius_type,
        valence_type,
        bond_depth.reshape(-1),
        pair_tiles.reshape(-1),
        tile_count.reshape(-1),
    )


def solution(mesh):
    in_specs = (
        P(None, ("row", "col")),
        P(("row", "col")),
        P(),
        P(),
        P(),
        P("row", "col", None, None),
        P("row", "col"),
    )
    out_specs = P(None, ("row", "col"))
    return jax.shard_map(local, mesh=mesh, in_specs=in_specs, out_specs=out_specs, check_vma=False)
```

profile of v0, /device:TPU:6, one launch (start us, length us, event | category | flops | bytes accessed | tf_op | source)
XLA Modules:
  0.0 90.5 jit_solution(7022748448331632911)
XLA Ops:
  0.0 0.8 copy.8
  0.8 0.0 copy-start
  0.8 0.7 reshape.14.tiles_ref
  2.1 0.0 copy-done
  2.1 0.6 reshape.13.depth_ref
  2.8 86.4 %shard_map.73 = f32[4,1024]{1,0:T(4,128)} custom-call(f32[3,1024]{1,0:T(4,128)} %pos_ref.1, s32[8,128]{1,0:T(8,128)} %bitcast.5, f32[5]{0:T(128)} %radius_ref.1, f32[5]{0:T(128)} %valence_ref.1, f32[25]{0:T(128)} %reshape.13.depth_ref, s32[192]{0:T(256)} %reshape.14.tiles_ref, s32[1]{0:T(128)} %bitcast.4.count_ref), custom_call_target="tpu_custom_call" | custom-call | tf_op jit(solution)/shard_map/pallas_call | solution.py:323
  89.2 1.3 %copy.11 = f32[4,1024]{1,0:T(4,128)} copy(f32[4,1024]{1,0:T(4,128)} %shard_map.73) | data formatting | bytes 32768
Async XLA Ops:
  0.8 1.4 %copy-start = (f32[5,5]{1,0:T(8,128)S(1)}, f32[5,5]{1,0:T(8,128)}, u32[]{:S(2)}) copy-start(f32[5,5]{1,0:T(8,128)} %param.11) | copy-start | bytes 304
where the time goes:
time: 90.7 us; the launch traced here: 90.5 us
  Pallas kernels  86.4 us (95%)
  local copies, waits for them, and re-layouts  3.42 us (4%)
    pallas_call x1, Pallas kernels, local(): pl.pallas_call(kernel, out_shape=jax.ShapeDtypeStruct((4, positions.shape...  86.4 us
    unnamed x4, local copies, waits for them, and re-layouts  2.1 us

commit v1 on v0

v1 whole, which is shorter than its diff:
```python
import functools

import jax
import jax.numpy as jnp
from jax import lax
from jax.experimental import pallas as pl
from jax.experimental.pallas import tpu as pltpu
from jax.sharding import PartitionSpec as P

TILE = 128
SLOTS = 96
EARLY = 36
CHIPS = 16
MESH = pl.DeviceIdType.MESH
F32 = jnp.float32
BF16 = jnp.bfloat16
LOG2E = 1.4426950408889634


def pieces(value):
    high = value.astype(BF16).astype(F32)
    rest = value - high
    middle = rest.astype(BF16).astype(F32)
    return high, middle, rest - middle


def by_type(types, table):
    value = jnp.full(types.shape, table[0], F32)
    for t in range(1, len(table)):
        value = jnp.where(types == F32(t), table[t], value)
    return value


def kernel(
    pos_ref, types_ref, radius_ref, valence_ref, depth_ref, tiles_ref, count_ref, out_ref,
    rows, cols, row_radius, row_u, col_u, pick_ref, wide, wide_u, col_w, buf_a, buf_b, onehot, parts, store,
    coord_part, coord_in, coord_sum, coord_rx, force_part, force_in, force_sum, force_rx,
    row_send, row_recv, col_send, col_recv, pair_send, pair_recv,
    c_send, c_recv, u_send, u_recv, v_send, v_recv, f_send, f_recv,
):
    r = lax.axis_index("row")
    c = lax.axis_index("col")
    core = lax.rem(c, 2)
    q = c // 2
    z, x = q // 4, lax.rem(q, 4)
    zh, y = r // 4, lax.rem(r, 4)
    other = 1 - core

    def copy(src, dst, send, recv, row, col):
        return pltpu.make_async_remote_copy(
            src_ref=src, dst_ref=dst, send_sem=send, recv_sem=recv,
            device_id=(row, col), device_id_type=MESH,
        )

    chips = [lax.rem(q + k, CHIPS) for k in range(1, CHIPS)]
    rows_of = [lax.rem(r + k, 8) for k in range(1, 8)]

    def device(zz, xx):
        return (zz * 4 + xx) * 2 + core

    far = [lax.rem(z + k, 4) for k in range(1, 4)]
    side = [lax.rem(x + k, 4) for k in range(1, 4)]
    yy = [lax.rem(y + k, 4) for k in range(1, 4)]
    partner = q * 2 + other
    twin = (1 - zh) * 4 + y
    greeted = [(twin, c)]
    greeted += [(r, device(zz, x)) for zz in far]
    greeted += [(r, device(z, xx)) for xx in side]
    greeted += [(zh * 4 + near, c) for near in yy]
    greeted += [(r, partner)]
    barrier = pltpu.get_barrier_semaphore()
    for row, col in greeted:
        pl.semaphore_signal(barrier, inc=1, device_id=(row, col), device_id_type=MESH)

    own_types = types_ref[...].astype(F32)
    for k in range(8):
        piece = pos_ref[:, k * TILE : (k + 1) * TILE]
        for d in range(3):
            rows[core, q, d, k : k + 1, :] = piece[d : d + 1]
            cols[r, d, k : k + 1, :] = piece[d : d + 1]
    rows[core, q, 3] = own_types
    cols[r, 3] = own_types

    sub = lax.broadcasted_iota(jnp.int32, (8, TILE), 0)
    blank = jnp.zeros((8, TILE), F32)
    for k in range(8):
        mark = jnp.where(sub == k, F32(1), F32(0))
        for d in range(4):
            column = [mark if 3 * d <= f < 3 * d + 3 else blank for f in range(16)]
            m = d * 8 + k
            at = slice(m % 2 * TILE, m % 2 * TILE + TILE)
            pick_ref[m // 2, :, at] = jnp.concatenate(column, axis=0).astype(BF16)

    pl.semaphore_wait(barrier, len(greeted))

    started = []

    def go(*args):
        descriptor = copy(*args)
        descriptor.start()
        started.append(descriptor)

    def send_row(origin, row, col, slot):
        block = rows.at[core, origin]
        go(block, block, row_send.at[slot], row_recv.at[core, origin], row, col)

    def send_col(origin, row, slot):
        block = cols.at[origin]
        go(block, block, col_send.at[slot], col_recv.at[origin], row, c)

    slot = 0
    send_col(r, twin, 0)
    for zz in far:
        send_row(q, r, device(zz, x), slot)
        slot += 1
    for xx in side:
        send_row(q, r, device(z, xx), slot)
        slot += 1
    for k, near in enumerate(yy):
        send_col(r, zh * 4 + near, 1 + k)
    send_row(q, r, partner, slot)
    slot += 1

    def row_wait(par, origin):
        block = rows.at[par, origin]
        copy(block, block, row_send.at[0], row_recv.at[par, origin], r, partner).wait_recv()

    def col_wait(origin):
        block = cols.at[origin]
        copy(block, block, col_send.at[0], col_recv.at[origin], twin, c).wait_recv()

    live = count_ref[0, 0]
    lane = lax.broadcasted_iota(jnp.int32, (8, TILE), 1) // 8
    target = lax.broadcasted_iota(jnp.int32, (256, TILE), 0)
    for m in range(SLOTS // 16):

        def pick(s, held, m=m):
            at = m * 16 + s
            a = tiles_ref[0, at]
            place = ((a >> 3) & 1) * 128 + (a >> 4) * 8 + (a & 7)
            place = jnp.where(at < live, place, -1)
            return jnp.where(lane == s, place, held)

        held = lax.fori_loop(0, 16, pick, jnp.full((8, TILE), -1, jnp.int32))
        match = target == held[0:1]
        onehot[:, m * TILE : (m + 1) * TILE] = jnp.where(match, F32(1), F32(0)).astype(BF16)

    radius = [radius_ref[t] * F32(0.5) for t in range(5)]
    valence = [valence_ref[t] for t in range(5)]

    def turn(feats):
        feats = feats + [blank] * (16 - len(feats))
        return jnp.concatenate(feats, axis=0).T.astype(BF16)

    def lanes_of(left, put_block):
        for m in range(16):
            pair = jnp.dot(left, pick_ref[m], preferred_element_type=F32)
            for h in range(2):
                put_block((2 * m + h) // 8, (2 * m + h) % 8, pair[:, h * TILE : (h + 1) * TILE].reshape(16, 8, TILE))

    def widen(g):
        feats = []
        for value in (cols[g, 0], cols[g, 1], cols[g, 2], by_type(cols[g, 3], radius)):
            feats.extend(pieces(value))

        def put_block(d, k, value):
            wide[g * 8 + k, :, d] = value

        lanes_of(turn(feats), put_block)

    for zz in far:
        origin = zz * 4 + x
        row_wait(core, origin)
        for xx in side:
            send_row(origin, r, device(z, xx), slot)
            slot += 1
        send_row(origin, r, partner, slot)
        slot += 1
    widen(r)
    col_wait(twin)
    for k, near in enumerate(yy):
        send_col(twin, zh * 4 + near, 4 + k)

    def relay(k):
        for xx in side:
            origin = lax.rem(z + k, 4) * 4 + xx
            row_wait(core, origin)
            send_row(origin, r, partner, slots.pop())

    slots = list(range(slot, slot + 12))
    relay(0)

    def near_cols(k, carry):
        origin = zh * 4 + lax.rem(y + k, 4)
        col_wait(origin)
        widen(origin)
        return carry

    lax.fori_loop(1, 4, near_cols, 0)
    for k in range(1, 4):
        relay(k)
    widen(twin)

    def far_cols(k, carry):
        origin = (1 - zh) * 4 + lax.rem(y + k, 4)
        col_wait(origin)
        widen(origin)
        return carry

    lax.fori_loop(1, 4, far_cols, 0)
    for p in range(CHIPS):
        row_wait(other, p)
    for par in range(2):
        for p in range(CHIPS):
            row_radius[par, p] = by_type(rows[par, p, 3], radius)

    def tile_of(s):
        a = tiles_ref[0, s]
        b = tiles_ref[1, s]
        return (a >> 3) & 1, a >> 4, a & 7, b

    def same_block(s):
        a = tiles_ref[0, s]
        b = tiles_ref[1, s]
        same = ((b >> 3) == r) & ((a >> 3) == c) & ((a & 7) == (b & 7))
        return jnp.where(same, F32(1), F32(0))

    def near_rows(s):
        sp, sq, sb, b = tile_of(s)
        near = [rows[sp, sq, d, pl.ds(sb, 1), :] for d in range(3)]
        return near, row_radius[sp, sq, pl.ds(sb, 1), :], b

    def over_tiles(fill, use, begin, end):
        fill(begin, buf_a)

        def body(t, carry):
            s = begin + 2 * t
            fill(s + 1, buf_b)
            use(s, buf_a)
            fill(jnp.minimum(s + 2, SLOTS - 1), buf_a)
            use(s + 1, buf_b)
            return carry

        lax.fori_loop(0, (end - begin) // 2, body, 0)

    def put(d, s, value):
        parts[d, pl.ds(pl.multiple_of(s * 8, 8), 8), :] = value

    def first(s, carry):
        near, near_r, b = near_rows(s)
        total = jnp.where(sub == 0, -same_block(s), F32(0))
        for k in range(16):
            dist = F32(0)
            for d in range(3):
                offset = near[d] - wide[b, k, d]
                dist = dist + offset * offset
            rho = near_r + wide[b, k, 3]
            ratio = dist / (rho * rho)
            total = total + jnp.exp2((ratio * ratio) * (ratio * F32(-LOG2E)))
        put(0, s, total)
        return carry

    lax.fori_loop(0, SLOTS, first, 0)

    def scatter(value):
        high = value.astype(BF16)
        low = (value - high.astype(F32)).astype(BF16)
        return high, low

    def spots(value):
        return value.reshape(2, CHIPS, 8, TILE)

    both = jnp.concatenate(scatter(parts[0]), axis=1)
    both = jnp.dot(onehot[...], both, preferred_element_type=F32)
    coord_part[...] = spots(both[:, :TILE] + both[:, TILE:])
    go(coord_part.at[other], coord_in, pair_send.at[0], pair_recv.at[0], r, partner)
    mine = coord_part[core]
    copy(coord_part.at[0], coord_in, pair_send.at[0], pair_recv.at[0], r, partner).wait_recv()
    coord_sum[...] = mine + coord_in[...]
    for k, p in enumerate(chips):
        go(coord_sum.at[p], coord_rx.at[q], c_send.at[k], c_recv.at[q], r, p * 2 + core)

    lane_at = lax.broadcasted_iota(jnp.int32, (8, TILE), 1)
    for g in range(8):
        feats = []
        for t in range(5):
            table = [depth_ref[t, u] * (valence[t] + valence[u]) for u in range(5)]
            feats.extend(pieces(by_type(cols[g, 3], table)))
        col_w[g] = turn(feats)

    def pair_terms(s, buf):
        sp, sq, sb, b = tile_of(s)
        kinds = jnp.broadcast_to(rows[sp, sq, 3, pl.ds(sb, 1), :], (8, TILE))
        kinds = jnp.where(sub == (b & 7), kinds, F32(-1))
        right = []
        for t in range(5):
            right.extend([jnp.where(kinds == F32(t), F32(1), F32(0))] * 3)
        right = jnp.concatenate(right + [blank], axis=0).astype(BF16)
        buf[...] = jnp.dot(col_w[b >> 3], right, preferred_element_type=F32)

    def prepare(s, buf):
        near, near_r, b = near_rows(s)
        same = same_block(s)
        for k in range(16):
            dx, dy, dz = (near[d] - wide[b, k, d] for d in range(3))
            rho = near_r + wide[b, k, 3]
            inverse = F32(1) / (rho * rho)
            ratio = (dx * dx + dy * dy + dz * dz) * inverse
            square = ratio * ratio
            numer = buf[8 * k : 8 * k + 8, :] * jnp.exp2(square * (ratio * F32(-LOG2E)))
            numer = jnp.where(lane_at == sub + 8 * k, numer * (F32(1) - same), numer)
            pull = numer * (square * inverse)
            store[s, k, 0] = pull * dx
            store[s, k, 1] = pull * dy
            store[s, k, 2] = pull * dz
            store[s, k, 3] = numer

    over_tiles(pair_terms, prepare, 0, EARLY)

    own = coord_sum[q]
    for p in chips:
        copy(coord_sum.at[0], coord_rx.at[p], c_send.at[0], c_recv.at[p], r, p * 2 + core).wait_recv()
        own = own + coord_rx[p]
    own = own + by_type(rows[core, q, 3], valence)
    row_u[core, q] = own
    col_u[r] = own
    for k, p in enumerate(rows_of):
        go(col_u.at[r], col_u.at[r], v_send.at[k], v_recv.at[r], p, c)
    for k, p in enumerate(chips):
        go(row_u.at[core, q], row_u.at[core, q], u_send.at[k], u_recv.at[q], r, p * 2 + core)

    over_tiles(pair_terms, prepare, EARLY, SLOTS)

    for p in chips:
        block = row_u.at[core, p]
        copy(block, block, u_send.at[0], u_recv.at[p], r, p * 2 + core).wait_recv()
    go(row_u.at[core], row_u.at[core], pair_send.at[1], pair_recv.at[1], r, partner)
    for p in rows_of:
        copy(col_u.at[p], col_u.at[p], v_send.at[0], v_recv.at[p], p, c).wait_recv()
    for g in range(2):
        feats = []
        for k in range(4):
            feats.extend(pieces(col_u[4 * g + k]))

        def put_u(d, k, value, g=g):
            wide_u[g * 32 + d * 8 + k] = value

        lanes_of(turn(feats), put_u)
    copy(row_u.at[other], row_u.at[other], pair_send.at[1], pair_recv.at[1], r, partner).wait_recv()

    def second(s, carry):
        sp, sq, sb, b = tile_of(s)
        near = row_u[sp, sq, pl.ds(sb, 1), :]
        total = [F32(0)] * 4
        for k in range(16):
            scale = F32(1) / (near + wide_u[b, k])
            for d in range(4):
                total[d] = total[d] + store[s, k, d] * scale
        for d in range(4):
            put(d, s, total[d])
        return carry

    lax.fori_loop(0, SLOTS, second, 0)

    for d in (0, 2):
        high, low = scatter(jnp.concatenate([parts[d], parts[d + 1]], axis=1))
        both = jnp.dot(onehot[...], high, preferred_element_type=F32)
        both = both + jnp.dot(onehot[...], low, preferred_element_type=F32)
        force_part[:, :, d] = spots(both[:, :TILE])
        force_part[:, :, d + 1] = spots(both[:, TILE:])
    go(force_part.at[other], force_in, pair_send.at[2], pair_recv.at[2], r, partner)
    copy(force_part.at[0], force_in, pair_send.at[2], pair_recv.at[2], r, partner).wait_recv()
    force_sum[...] = force_part[core] + force_in[...]
    for k, p in enumerate(chips):
        go(force_sum.at[p], force_rx.at[q], f_send.at[k], f_recv.at[q], r, p * 2 + core)
    own = force_sum[q]
    for p in chips:
        copy(force_sum.at[0], force_rx.at[p], f_send.at[0], f_recv.at[p], r, p * 2 + core).wait_recv()
        own = own + force_rx[p]
    for k in range(8):
        out_ref[:, k * TILE : (k + 1) * TILE] = own[:, k, :]
    for descriptor in started:
        descriptor.wait_send()


def local(positions, types, radius_type, valence_type, bond_depth, pair_tiles, tile_count):
    vmem = pl.BlockSpec(memory_space=pltpu.VMEM)
    smem = pl.BlockSpec(memory_space=pltpu.SMEM)
    dma = pltpu.SemaphoreType.DMA
    sums = pl.pallas_call(
        kernel,
        out_shape=jax.ShapeDtypeStruct((4, positions.shape[1]), F32),
        in_specs=[vmem, vmem, smem, smem, smem, smem, smem],
        out_specs=vmem,
        scratch_shapes=[
            pltpu.VMEM((2, CHIPS, 4, 8, TILE), F32),
            pltpu.VMEM((8, 4, 8, TILE), F32),
            pltpu.VMEM((2, CHIPS, 8, TILE), F32),
            pltpu.VMEM((2, CHIPS, 8, TILE), F32),
            pltpu.VMEM((8, 8, TILE), F32),
            pltpu.VMEM((16, TILE, 2 * TILE), BF16),
            pltpu.VMEM((64, 16, 4, 8, TILE), F32),
            pltpu.VMEM((64, 16, 8, TILE), F32),
            pltpu.VMEM((8, TILE, TILE), BF16),
            pltpu.VMEM((TILE, TILE), F32),
            pltpu.VMEM((TILE, TILE), F32),
            pltpu.VMEM((256, 8 * SLOTS), BF16),
            pltpu.VMEM((4, 8 * SLOTS, TILE), F32),
            pltpu.VMEM((SLOTS, 16, 4, 8, TILE), F32),
            pltpu.VMEM((2, CHIPS, 8, TILE), F32),
            pltpu.VMEM((CHIPS, 8, TILE), F32),
            pltpu.VMEM((CHIPS, 8, TILE), F32),
            pltpu.VMEM((CHIPS, 8, TILE), F32),
            pltpu.VMEM((2, CHIPS, 4, 8, TILE), F32),
            pltpu.VMEM((CHIPS, 4, 8, TILE), F32),
            pltpu.VMEM((CHIPS, 4, 8, TILE), F32),
            pltpu.VMEM((CHIPS, 4, 8, TILE), F32),
            dma((31,)), dma((2, CHIPS)), dma((7,)), dma((8,)), dma((3,)), dma((3,)),
            dma((15,)), dma((CHIPS,)), dma((15,)), dma((CHIPS,)), dma((7,)), dma((8,)),
            dma((15,)), dma((CHIPS,)),
        ],
        compiler_params=pltpu.CompilerParams(
            collective_id=0, has_side_effects=True, vmem_limit_bytes=54 * 1024 * 1024
        ),
    )(
        positions,
        types.reshape(8, TILE),
        radius_type,
        valence_type,
        bond_depth,
        pair_tiles.reshape(SLOTS, 2).T,
        tile_count,
    )
    component = lax.broadcasted_iota(jnp.int32, sums.shape, 0)
    return jnp.where(component < 3, F32(-6), F32(-1)) * sums


def solution(mesh):
    in_specs = (
        P(None, ("row", "col")),
        P(("row", "col")),
        P(),
        P(),
        P(),
        P("row", "col", None, None),
        P("row", "col"),
    )
    out_specs = P(None, ("row", "col"))
    return jax.shard_map(local, mesh=mesh, in_specs=in_specs, out_specs=out_specs, check_vma=False)
```

time: 90.7 us -> 55.1 us (0.61)
  Pallas kernels: 86.4 us -> 52.8 us
  local copies, waits for them, and re-layouts: 3.42 us -> 0 us
  other arithmetic: 0 us -> 1.4 us
    pallas_call x1, Pallas kernels: 86.4 us -> 52.8 us  [local(): pl.pallas_call(kernel, out_shape=jax.ShapeDtypeStruct((4, positions.shape...]
    unnamed x4 -> x0, local copies, waits for them, and re-layouts: 2.1 us -> none
    mul x0 -> x1, other arithmetic: none -> 1.39 us  [local(): return jnp.where(component < 3, F32(-6), F32(-1)) * sums]
    reshape x2 -> x0, local copies, waits for them, and re-layouts: 1.32 us -> none  [the longest x1 0.7 us: local(): pair_tiles.reshape(-1)]
where the time goes in v1:
time: 55.1 us; the launch traced here: 54.8 us
  Pallas kernels  52.8 us (96%)
  other arithmetic  1.4 us (3%)
  between operations  0.67 us (1%)
    pallas_call x1, Pallas kernels, local(): pl.pallas_call(kernel, out_shape=jax.ShapeDtypeStruct((4, positions.shape...  52.8 us
    mul x1, other arithmetic, local(): return jnp.where(component < 3, F32(-6), F32(-1)) * sums  1.39 us

profile of v1, /device:TPU:6, one launch (start us, length us, event | category | flops | bytes accessed | tf_op | source)
XLA Modules:
  0.0 54.8 jit_solution(1654036977320295587)
XLA Ops:
  0.7 52.8 %shard_map.73 = f32[4,1024]{1,0:T(4,128)} custom-call(f32[3,1024]{1,0:T(4,128)} %pos_ref.1, s32[8,128]{1,0:T(8,128)} %bitcast.4, f32[5]{0:T(128)} %radius_ref.1, f32[5]{0:T(128)} %valence_ref.1, f32[5,5]{1,0:T(8,128)} %depth_ref.1, s32[2,96]{1,0:T(2,128)} %bitcast.5, s32[1,1]{1,0:T(1,128)S(6)} %copy.8.count_ref), custom_call_target="tpu_custom_call" | custom-call | tf_op jit(solution)/shard_map/pallas_call | solution.py:390
  53.4 1.4 %broadcast_multiply_fusion = f32[4,1024]{1,0:T(4,128)} fusion(f32[4,1024]{1,0:T(4,128)} %shard_map.73, f32[4]{0:T(128)S(1)} %compare_select_fusion), kind=kLoop, calls=%fused_computation | loop fusion | flops 4096 | bytes 32784 | tf_op jit(solution)/shard_map/mul | solution.py:435
  (1 shorter events, 0.0 us)

commit v2 on v1

--- a/solution.py
+++ b/solution.py
@@ -11,6 +11,7 @@
 SLOTS = 96
 EARLY = 36
 CHIPS = 16
+VMEM = 56 * 1024 * 1024
 MESH = pl.DeviceIdType.MESH
 F32 = jnp.float32
 BF16 = jnp.bfloat16
@@ -32,9 +33,10 @@
 
 
 def kernel(
-    pos_ref, types_ref, radius_ref, valence_ref, depth_ref, tiles_ref, count_ref, out_ref,
+    pos_in, types_in, radius_in, valence_in, depth_in, tiles_in, count_in, out_ref,
+    pos_ref, types_ref, radius_ref, valence_ref, depth_ref, tiles_ref, count_ref, load_sem,
     rows, cols, row_radius, row_u, col_u, pick_ref, wide, wide_u, col_w, buf_a, buf_b, onehot, parts, store,
-    coord_part, coord_in, coord_sum, coord_rx, force_part, force_in, force_sum, force_rx,
+    coord_part, coord_rx, force_out, force_in, force_sum, force_rx,
     row_send, row_recv, col_send, col_recv, pair_send, pair_recv,
     c_send, c_recv, u_send, u_recv, v_send, v_recv, f_send, f_recv,
 ):
@@ -69,17 +71,14 @@
     greeted += [(zh * 4 + near, c) for near in yy]
     greeted += [(r, partner)]
     barrier = pltpu.get_barrier_semaphore()
+    inputs = (pos_in, types_in, radius_in, valence_in, depth_in, tiles_in, count_in)
+    locals_ = (pos_ref, types_ref, radius_ref, valence_ref, depth_ref, tiles_ref, count_ref)
+    loads = [pltpu.make_async_copy(a, b, load_sem.at[k]) for k, (a, b) in enumerate(zip(inputs, locals_))]
+    for load in loads:
+        load.start()
+
     for row, col in greeted:
         pl.semaphore_signal(barrier, inc=1, device_id=(row, col), device_id_type=MESH)
-
-    own_types = types_ref[...].astype(F32)
-    for k in range(8):
-        piece = pos_ref[:, k * TILE : (k + 1) * TILE]
-        for d in range(3):
-            rows[core, q, d, k : k + 1, :] = piece[d : d + 1]
-            cols[r, d, k : k + 1, :] = piece[d : d + 1]
-    rows[core, q, 3] = own_types
-    cols[r, 3] = own_types
 
     sub = lax.broadcasted_iota(jnp.int32, (8, TILE), 0)
     blank = jnp.zeros((8, TILE), F32)
@@ -91,6 +90,17 @@
             at = slice(m % 2 * TILE, m % 2 * TILE + TILE)
             pick_ref[m // 2, :, at] = jnp.concatenate(column, axis=0).astype(BF16)
 
+    for load in loads:
+        load.wait()
+    own_types = types_ref[...].astype(F32)
+    for k in range(8):
+        piece = pos_ref[:, k * TILE : (k + 1) * TILE]
+        for d in range(3):
+            rows[core, q, d, k : k + 1, :] = piece[d : d + 1]
+            cols[r, d, k : k + 1, :] = piece[d : d + 1]
+    rows[core, q, 3] = own_types
+    cols[r, 3] = own_types
+
     pl.semaphore_wait(barrier, len(greeted))
 
     started = []
@@ -108,18 +118,14 @@
         block = cols.at[origin]
         go(block, block, col_send.at[slot], col_recv.at[origin], row, c)
 
-    slot = 0
     send_col(r, twin, 0)
-    for zz in far:
-        send_row(q, r, device(zz, x), slot)
-        slot += 1
-    for xx in side:
-        send_row(q, r, device(z, xx), slot)
-        slot += 1
+    for k, zz in enumerate(far):
+        send_row(q, r, device(zz, x), k)
+    for k, xx in enumerate(side):
+        send_row(q, r, device(z, xx), 3 + k)
     for k, near in enumerate(yy):
         send_col(r, zh * 4 + near, 1 + k)
-    send_row(q, r, partner, slot)
-    slot += 1
+    send_row(q, r, partner, 6)
 
     def row_wait(par, origin):
         block = rows.at[par, origin]
@@ -130,20 +136,18 @@
         copy(block, block, col_send.at[0], col_recv.at[origin], twin, c).wait_recv()
 
     live = count_ref[0, 0]
-    lane = lax.broadcasted_iota(jnp.int32, (8, TILE), 1) // 8
-    target = lax.broadcasted_iota(jnp.int32, (256, TILE), 0)
-    for m in range(SLOTS // 16):
-
-        def pick(s, held, m=m):
-            at = m * 16 + s
-            a = tiles_ref[0, at]
-            place = ((a >> 3) & 1) * 128 + (a >> 4) * 8 + (a & 7)
-            place = jnp.where(at < live, place, -1)
-            return jnp.where(lane == s, place, held)
-
-        held = lax.fori_loop(0, 16, pick, jnp.full((8, TILE), -1, jnp.int32))
-        match = target == held[0:1]
-        onehot[:, m * TILE : (m + 1) * TILE] = jnp.where(match, F32(1), F32(0)).astype(BF16)
+    lane_at = lax.broadcasted_iota(jnp.int32, (8, TILE), 1)
+
+    def place_of(at, held):
+        a = tiles_ref[0, at]
+        place = ((a >> 3) & 1) * 128 + (a >> 4) * 8 + (a & 7)
+        return jnp.where((lane_at == at) & (at < live), place, held)
+
+    held = lax.fori_loop(0, SLOTS, place_of, jnp.full((8, TILE), -1, jnp.int32))
+    match = lax.broadcasted_iota(jnp.int32, (256, TILE), 0) == held[0:1]
+    onehot[...] = jnp.where(match, F32(1), F32(0)).astype(BF16)
+    for d in range(4):
+        parts[d, SLOTS:TILE, :] = jnp.zeros((TILE - SLOTS, TILE), F32)
 
     radius = [radius_ref[t] * F32(0.5) for t in range(5)]
     valence = [valence_ref[t] for t in range(5)]
@@ -168,27 +172,24 @@
 
         lanes_of(turn(feats), put_block)
 
-    for zz in far:
+    for k, zz in enumerate(far):
         origin = zz * 4 + x
         row_wait(core, origin)
-        for xx in side:
-            send_row(origin, r, device(z, xx), slot)
-            slot += 1
-        send_row(origin, r, partner, slot)
-        slot += 1
+        for j, xx in enumerate(side):
+            send_row(origin, r, device(z, xx), 7 + 4 * k + j)
+        send_row(origin, r, partner, 10 + 4 * k)
+
+    def relay(k, slot):
+        for j, xx in enumerate(side):
+            origin = lax.rem(z + k, 4) * 4 + xx
+            row_wait(core, origin)
+            send_row(origin, r, partner, slot + j)
+
     widen(r)
     col_wait(twin)
     for k, near in enumerate(yy):
         send_col(twin, zh * 4 + near, 4 + k)
-
-    def relay(k):
-        for xx in side:
-            origin = lax.rem(z + k, 4) * 4 + xx
-            row_wait(core, origin)
-            send_row(origin, r, partner, slots.pop())
-
-    slots = list(range(slot, slot + 12))
-    relay(0)
+    relay(0, 19)
 
     def near_cols(k, carry):
         origin = zh * 4 + lax.rem(y + k, 4)
@@ -198,7 +199,7 @@
 
     lax.fori_loop(1, 4, near_cols, 0)
     for k in range(1, 4):
-        relay(k)
+        relay(k, 19 + 3 * k)
     widen(twin)
 
     def far_cols(k, carry):
@@ -244,9 +245,9 @@
         lax.fori_loop(0, (end - begin) // 2, body, 0)
 
     def put(d, s, value):
-        parts[d, pl.ds(pl.multiple_of(s * 8, 8), 8), :] = value
-
-    def first(s, carry):
+        parts[d, pl.ds(s, 1), :] = jnp.sum(value, axis=0, keepdims=True)
+
+    def first(s):
         near, near_r, b = near_rows(s)
         total = jnp.where(sub == 0, -same_block(s), F32(0))
         for k in range(16):
@@ -258,9 +259,16 @@
             ratio = dist / (rho * rho)
             total = total + jnp.exp2((ratio * ratio) * (ratio * F32(-LOG2E)))
         put(0, s, total)
-        return carry
-
-    lax.fori_loop(0, SLOTS, first, 0)
+
+    def by_fours(use):
+        def body(t, carry):
+            for k in range(4):
+                use(4 * t + k)
+            return carry
+
+        lax.fori_loop(0, SLOTS // 4, body, 0)
+
+    by_fours(first)
 
     def scatter(value):
         high = value.astype(BF16)
@@ -273,14 +281,10 @@
     both = jnp.concatenate(scatter(parts[0]), axis=1)
     both = jnp.dot(onehot[...], both, preferred_element_type=F32)
     coord_part[...] = spots(both[:, :TILE] + both[:, TILE:])
-    go(coord_part.at[other], coord_in, pair_send.at[0], pair_recv.at[0], r, partner)
-    mine = coord_part[core]
-    copy(coord_part.at[0], coord_in, pair_send.at[0], pair_recv.at[0], r, partner).wait_recv()
-    coord_sum[...] = mine + coord_in[...]
-    for k, p in enumerate(chips):
-        go(coord_sum.at[p], coord_rx.at[q], c_send.at[k], c_recv.at[q], r, p * 2 + core)
-
-    lane_at = lax.broadcasted_iota(jnp.int32, (8, TILE), 1)
+    peers = [(par, p) for p in chips for par in (core, other)] + [(other, q)]
+    for k, (par, p) in enumerate(peers):
+        go(coord_part.at[par, p], coord_rx.at[core, q], c_send.at[k], c_recv.at[core, q], r, p * 2 + par)
+
     for g in range(8):
         feats = []
         for t in range(5):
@@ -317,10 +321,11 @@
 
     over_tiles(pair_terms, prepare, 0, EARLY)
 
-    own = coord_sum[q]
-    for p in chips:
-        copy(coord_sum.at[0], coord_rx.at[p], c_send.at[0], c_recv.at[p], r, p * 2 + core).wait_recv()
-        own = own + coord_rx[p]
+    own = coord_part[core, q]
+    for par, p in peers:
+        block = coord_rx.at[par, p]
+        copy(block, block, c_send.at[0], c_recv.at[par, p], r, p * 2 + par).wait_recv()
+        own = own + coord_rx[par, p]
     own = own + by_type(rows[core, q, 3], valence)
     row_u[core, q] = own
     col_u[r] = own
@@ -335,20 +340,23 @@
         block = row_u.at[core, p]
         copy(block, block, u_send.at[0], u_recv.at[p], r, p * 2 + core).wait_recv()
     go(row_u.at[core], row_u.at[core], pair_send.at[1], pair_recv.at[1], r, partner)
-    for p in rows_of:
-        copy(col_u.at[p], col_u.at[p], v_send.at[0], v_recv.at[p], p, c).wait_recv()
-    for g in range(2):
+    for side_of in (zh, 1 - zh):
+        for k in range(4):
+            p = side_of * 4 + lax.rem(y + k, 4)
+            if side_of is zh and k == 0:
+                continue
+            copy(col_u.at[p], col_u.at[p], v_send.at[0], v_recv.at[p], p, c).wait_recv()
         feats = []
         for k in range(4):
-            feats.extend(pieces(col_u[4 * g + k]))
-
-        def put_u(d, k, value, g=g):
-            wide_u[g * 32 + d * 8 + k] = value
+            feats.extend(pieces(col_u[4 * side_of + k]))
+
+        def put_u(d, k, value, side_of=side_of):
+            wide_u[side_of * 32 + d * 8 + k] = value
 
         lanes_of(turn(feats), put_u)
     copy(row_u.at[other], row_u.at[other], pair_send.at[1], pair_recv.at[1], r, partner).wait_recv()
 
-    def second(s, carry):
+    def second(s):
         sp, sq, sb, b = tile_of(s)
         near = row_u[sp, sq, pl.ds(sb, 1), :]
         total = [F32(0)] * 4
@@ -358,19 +366,24 @@
                 total[d] = total[d] + store[s, k, d] * scale
         for d in range(4):
             put(d, s, total[d])
-        return carry
-
-    lax.fori_loop(0, SLOTS, second, 0)
-
-    for d in (0, 2):
-        high, low = scatter(jnp.concatenate([parts[d], parts[d + 1]], axis=1))
-        both = jnp.dot(onehot[...], high, preferred_element_type=F32)
-        both = both + jnp.dot(onehot[...], low, preferred_element_type=F32)
-        force_part[:, :, d] = spots(both[:, :TILE])
-        force_part[:, :, d + 1] = spots(both[:, TILE:])
-    go(force_part.at[other], force_in, pair_send.at[2], pair_recv.at[2], r, partner)
-    copy(force_part.at[0], force_in, pair_send.at[2], pair_recv.at[2], r, partner).wait_recv()
-    force_sum[...] = force_part[core] + force_in[...]
+
+    by_fours(second)
+
+    sums = [scatter(jnp.concatenate([parts[d], parts[d + 1]], axis=1)) for d in (0, 2)]
+
+    def gathered(par, ref):
+        chosen = onehot[pl.ds(pl.multiple_of(par * TILE, TILE), TILE), :]
+        for d, (high, low) in zip((0, 2), sums):
+            both = jnp.dot(chosen, high, preferred_element_type=F32)
+            both = both + jnp.dot(chosen, low, preferred_element_type=F32)
+            ref[:, d] = both[:, :TILE].reshape(CHIPS, 8, TILE)
+            ref[:, d + 1] = both[:, TILE:].reshape(CHIPS, 8, TILE)
+
+    gathered(other, force_out)
+    go(force_out, force_in, pair_send.at[2], pair_recv.at[2], r, partner)
+    gathered(core, force_sum)
+    copy(force_out, force_in, pair_send.at[2], pair_recv.at[2], r, partner).wait_recv()
+    force_sum[...] = force_sum[...] + force_in[...]
     for k, p in enumerate(chips):
         go(force_sum.at[p], force_rx.at[q], f_send.at[k], f_recv.at[q], r, p * 2 + core)
     own = force_sum[q]
@@ -385,14 +398,22 @@
 
 def local(positions, types, radius_type, valence_type, bond_depth, pair_tiles, tile_count):
     vmem = pl.BlockSpec(memory_space=pltpu.VMEM)
-    smem = pl.BlockSpec(memory_space=pltpu.SMEM)
+    smem = pltpu.SMEM
     dma = pltpu.SemaphoreType.DMA
     sums = pl.pallas_call(
         kernel,
         out_shape=jax.ShapeDtypeStruct((4, positions.shape[1]), F32),
-        in_specs=[vmem, vmem, smem, smem, smem, smem, smem],
+        in_specs=[pl.BlockSpec(memory_space=pltpu.HBM)] * 7,
         out_specs=vmem,
         scratch_shapes=[
+            pltpu.VMEM(positions.shape, F32),
+            pltpu.VMEM((8, TILE), jnp.int32),
+            smem(radius_type.shape, F32),
+            smem(valence_type.shape, F32),
+            smem(bond_depth.shape, F32),
+            smem((2, SLOTS), jnp.int32),
+            smem((1, 1), jnp.int32),
+            dma((7,)),
             pltpu.VMEM((2, CHIPS, 4, 8, TILE), F32),
             pltpu.VMEM((8, 4, 8, TILE), F32),
             pltpu.VMEM((2, CHIPS, 8, TILE), F32),
@@ -404,23 +425,21 @@
             pltpu.VMEM((8, TILE, TILE), BF16),
             pltpu.VMEM((TILE, TILE), F32),
             pltpu.VMEM((TILE, TILE), F32),
-            pltpu.VMEM((256, 8 * SLOTS), BF16),
-            pltpu.VMEM((4, 8 * SLOTS, TILE), F32),
+            pltpu.VMEM((256, TILE), BF16),
+            pltpu.VMEM((4, TILE, TILE), F32),
             pltpu.VMEM((SLOTS, 16, 4, 8, TILE), F32),
             pltpu.VMEM((2, CHIPS, 8, TILE), F32),
-            pltpu.VMEM((CHIPS, 8, TILE), F32),
-            pltpu.VMEM((CHIPS, 8, TILE), F32),
-            pltpu.VMEM((CHIPS, 8, TILE), F32),
-            pltpu.VMEM((2, CHIPS, 4, 8, TILE), F32),
+            pltpu.VMEM((2, CHIPS, 8, TILE), F32),
+            pltpu.VMEM((CHIPS, 4, 8, TILE), F32),
             pltpu.VMEM((CHIPS, 4, 8, TILE), F32),
             pltpu.VMEM((CHIPS, 4, 8, TILE), F32),
             pltpu.VMEM((CHIPS, 4, 8, TILE), F32),
             dma((31,)), dma((2, CHIPS)), dma((7,)), dma((8,)), dma((3,)), dma((3,)),
-            dma((15,)), dma((CHIPS,)), dma((15,)), dma((CHIPS,)), dma((7,)), dma((8,)),
+            dma((31,)), dma((2, CHIPS)), dma((15,)), dma((CHIPS,)), dma((7,)), dma((8,)),
             dma((15,)), dma((CHIPS,)),
         ],
         compiler_params=pltpu.CompilerParams(
-            collective_id=0, has_side_effects=True, vmem_limit_bytes=54 * 1024 * 1024
+            collective_id=0, has_side_effects=True, vmem_limit_bytes=VMEM
         ),
     )(
         positions,

time: 55.1 us -> 52.6 us (0.955)
  Pallas kernels: 52.8 us -> 50.1 us
    pallas_call x1, Pallas kernels: 52.8 us -> 50.1 us  [local(): pl.pallas_call(kernel, out_shape=jax.ShapeDtypeStruct((4, positions.shape...]
where the time goes in v2:
time: 52.6 us; the launch traced here: 52.1 us
  Pallas kernels  50.1 us (95%)
  other arithmetic  1.4 us (3%)
  between operations  0.67 us (1%)
    pallas_call x1, Pallas kernels, local(): pl.pallas_call(kernel, out_shape=jax.ShapeDtypeStruct((4, positions.shape...  50.1 us
    mul x1, other arithmetic, local(): return jnp.where(component < 3, F32(-6), F32(-1)) * sums  1.39 us

profile of v2, /device:TPU:6, one launch (start us, length us, event | category | flops | bytes accessed | tf_op | source)
XLA Modules:
  0.0 52.1 jit_solution(7032491184628704842)
XLA Ops:
  0.7 50.1 %shard_map.73 = f32[4,1024]{1,0:T(4,128)} custom-call(f32[3,1024]{1,0:T(4,128)} %pos_in.1, s32[8,128]{1,0:T(8,128)} %bitcast.4, f32[5]{0:T(128)} %radius_in.1, f32[5]{0:T(128)} %valence_in.1, f32[5,5]{1,0:T(8,128)} %depth_in.1, s32[2,96]{1,0:T(2,128)} %bitcast.5, s32[1,1]{1,0:T(1,128)S(6)} %copy.8.count_in), custom_call_target="tpu_custom_call" | custom-call | tf_op jit(solution)/shard_map/pallas_call | solution.py:403
  50.7 1.4 %broadcast_multiply_fusion = f32[4,1024]{1,0:T(4,128)} fusion(f32[4,1024]{1,0:T(4,128)} %shard_map.73, f32[4]{0:T(128)S(1)} %compare_select_fusion), kind=kLoop, calls=%fused_computation | loop fusion | flops 4096 | bytes 32784 | tf_op jit(solution)/shard_map/mul | solution.py:454
  (1 shorter events, 0.0 us)

commit v3 on v2

--- a/solution.py
+++ b/solution.py
@@ -60,7 +60,8 @@
     def device(zz, xx):
         return (zz * 4 + xx) * 2 + core
 
-    far = [lax.rem(z + k, 4) for k in range(1, 4)]
+    half = z // 2
+    far = [z + 1 - 2 * lax.rem(z, 2), 2 - half, 3 * (1 - half)]
     side = [lax.rem(x + k, 4) for k in range(1, 4)]
     yy = [lax.rem(y + k, 4) for k in range(1, 4)]
     partner = q * 2 + other
@@ -119,7 +120,7 @@
         go(block, block, col_send.at[slot], col_recv.at[origin], row, c)
 
     send_col(r, twin, 0)
-    for k, zz in enumerate(far):
+    for k, zz in enumerate(far[::-1]):
         send_row(q, r, device(zz, x), k)
     for k, xx in enumerate(side):
         send_row(q, r, device(z, xx), 3 + k)
@@ -181,7 +182,7 @@
 
     def relay(k, slot):
         for j, xx in enumerate(side):
-            origin = lax.rem(z + k, 4) * 4 + xx
+            origin = [z, *far][k] * 4 + xx
             row_wait(core, origin)
             send_row(origin, r, partner, slot + j)
 

time: 52.6 us -> 52.2 us (level)
  no operation moved by 1% of the time
where the time goes in v3:
time: 52.2 us; the launch traced here: 51.9 us
  Pallas kernels  49.8 us (95%)
  other arithmetic  1.4 us (3%)
  between operations  0.67 us (1%)
    pallas_call x1, Pallas kernels, local(): pl.pallas_call(kernel, out_shape=jax.ShapeDtypeStruct((4, positions.shape...  49.8 us
    mul x1, other arithmetic, local(): return jnp.where(component < 3, F32(-6), F32(-1)) * sums  1.39 us

profile of v3, /device:TPU:6, one launch (start us, length us, event | category | flops | bytes accessed | tf_op | source)
XLA Modules:
  0.0 51.9 jit_solution(13769134049755686676)
XLA Ops:
  0.7 49.8 %shard_map.73 = f32[4,1024]{1,0:T(4,128)} custom-call(f32[3,1024]{1,0:T(4,128)} %pos_in.1, s32[8,128]{1,0:T(8,128)} %bitcast.4, f32[5]{0:T(128)} %radius_in.1, f32[5]{0:T(128)} %valence_in.1, f32[5,5]{1,0:T(8,128)} %depth_in.1, s32[2,96]{1,0:T(2,128)} %bitcast.5, s32[1,1]{1,0:T(1,128)S(6)} %copy.8.count_in), custom_call_target="tpu_custom_call" | custom-call | tf_op jit(solution)/shard_map/pallas_call | solution.py:404
  50.5 1.4 %broadcast_multiply_fusion = f32[4,1024]{1,0:T(4,128)} fusion(f32[4,1024]{1,0:T(4,128)} %shard_map.73, f32[4]{0:T(128)S(1)} %compare_select_fusion), kind=kLoop, calls=%fused_computation | loop fusion | flops 4096 | bytes 32784 | tf_op jit(solution)/shard_map/mul | solution.py:455
  (1 shorter events, 0.0 us)

commit v4 on v3

--- a/solution.py
+++ b/solution.py
@@ -261,15 +261,15 @@
             total = total + jnp.exp2((ratio * ratio) * (ratio * F32(-LOG2E)))
         put(0, s, total)
 
-    def by_fours(use):
+    def by_eights(use):
         def body(t, carry):
-            for k in range(4):
-                use(4 * t + k)
+            for k in range(8):
+                use(8 * t + k)
             return carry
 
-        lax.fori_loop(0, SLOTS // 4, body, 0)
-
-    by_fours(first)
+        lax.fori_loop(0, SLOTS // 8, body, 0)
+
+    by_eights(first)
 
     def scatter(value):
         high = value.astype(BF16)
@@ -368,7 +368,7 @@
         for d in range(4):
             put(d, s, total[d])
 
-    by_fours(second)
+    by_eights(second)
 
     sums = [scatter(jnp.concatenate([parts[d], parts[d + 1]], axis=1)) for d in (0, 2)]
 

time: 52.2 us -> 51.6 us (0.989)
    pallas_call x1, Pallas kernels: 49.8 us -> 49.3 us  [local(): pl.pallas_call(kernel, out_shape=jax.ShapeDtypeStruct((4, positions.shape...]
where the time goes in v4:
time: 51.6 us; the launch traced here: 51.3 us
  Pallas kernels  49.3 us (96%)
  other arithmetic  1.4 us (3%)
  between operations  0.67 us (1%)
    pallas_call x1, Pallas kernels, local(): pl.pallas_call(kernel, out_shape=jax.ShapeDtypeStruct((4, positions.shape...  49.3 us
    mul x1, other arithmetic, local(): return jnp.where(component < 3, F32(-6), F32(-1)) * sums  1.39 us

profile of v4, /device:TPU:6, one launch (start us, length us, event | category | flops | bytes accessed | tf_op | source)
XLA Modules:
  0.0 51.3 jit_solution(6551040483546245920)
XLA Ops:
  0.7 49.3 %shard_map.73 = f32[4,1024]{1,0:T(4,128)} custom-call(f32[3,1024]{1,0:T(4,128)} %pos_in.1, s32[8,128]{1,0:T(8,128)} %bitcast.4, f32[5]{0:T(128)} %radius_in.1, f32[5]{0:T(128)} %valence_in.1, f32[5,5]{1,0:T(8,128)} %depth_in.1, s32[2,96]{1,0:T(2,128)} %bitcast.5, s32[1,1]{1,0:T(1,128)S(6)} %copy.8.count_in), custom_call_target="tpu_custom_call" | custom-call | tf_op jit(solution)/shard_map/pallas_call | solution.py:404
  50.0 1.4 %broadcast_multiply_fusion = f32[4,1024]{1,0:T(4,128)} fusion(f32[4,1024]{1,0:T(4,128)} %shard_map.73, f32[4]{0:T(128)S(1)} %compare_select_fusion), kind=kLoop, calls=%fused_computation | loop fusion | flops 4096 | bytes 32784 | tf_op jit(solution)/shard_map/mul | solution.py:455
  (1 shorter events, 0.0 us)

commit v5 on v4

--- a/solution.py
+++ b/solution.py
@@ -62,7 +62,7 @@
 
     half = z // 2
     far = [z + 1 - 2 * lax.rem(z, 2), 2 - half, 3 * (1 - half)]
-    side = [lax.rem(x + k, 4) for k in range(1, 4)]
+    side = [lax.rem(x + k, 4) for k in (2, 1, 3)]
     yy = [lax.rem(y + k, 4) for k in range(1, 4)]
     partner = q * 2 + other
     twin = (1 - zh) * 4 + y

time: 51.6 us -> 51.6 us (level)
  no operation moved by 1% of the time
where the time goes in v5:
time: 51.6 us; the launch traced here: 51.4 us
  Pallas kernels  49.3 us (96%)
  other arithmetic  1.4 us (3%)
  between operations  0.67 us (1%)
    pallas_call x1, Pallas kernels, local(): pl.pallas_call(kernel, out_shape=jax.ShapeDtypeStruct((4, positions.shape...  49.3 us
    mul x1, other arithmetic, local(): return jnp.where(component < 3, F32(-6), F32(-1)) * sums  1.39 us

profile of v5, /device:TPU:6, one launch (start us, length us, event | category | flops | bytes accessed | tf_op | source)
XLA Modules:
  0.0 51.4 jit_solution(6102150250667168199)
XLA Ops:
  0.7 49.3 %shard_map.73 = f32[4,1024]{1,0:T(4,128)} custom-call(f32[3,1024]{1,0:T(4,128)} %pos_in.1, s32[8,128]{1,0:T(8,128)} %bitcast.4, f32[5]{0:T(128)} %radius_in.1, f32[5]{0:T(128)} %valence_in.1, f32[5,5]{1,0:T(8,128)} %depth_in.1, s32[2,96]{1,0:T(2,128)} %bitcast.5, s32[1,1]{1,0:T(1,128)S(6)} %copy.8.count_in), custom_call_target="tpu_custom_call" | custom-call | tf_op jit(solution)/shard_map/pallas_call | solution.py:404
  50.0 1.4 %broadcast_multiply_fusion = f32[4,1024]{1,0:T(4,128)} fusion(f32[4,1024]{1,0:T(4,128)} %shard_map.73, f32[4]{0:T(128)S(1)} %compare_select_fusion), kind=kLoop, calls=%fused_computation | loop fusion | flops 4096 | bytes 32784 | tf_op jit(solution)/shard_map/mul | solution.py:455
  (1 shorter events, 0.0 us)
